TPU v7x, 32 devices: a whole 2x2x4 slice. The times are simulated.
32 devices in a mesh: wide: 16 (over z, y, x), narrow: 2 (over core).
Axes of the slice: x: 2, y: 2, z: 4, core: 2. Of those that a mesh axis runs over, the one named last changes fastest.
Arguments:
- features: bfloat16 [512, 16384], P('wide', 'narrow'), may hold values from -6 to 6
- queries: bfloat16 [1024, 16384], P('wide', 'narrow'), may hold values from -6 to 6
- damping: float32 [16384], P('wide'), may hold values from 0.25 to 4
Outputs:
- kernel: float32 [16384, 16384], P('wide', 'narrow')
- factor: float32 [16384, 256], P('wide')
- scores: float32 [1024, 512], P('wide', 'narrow')
All inputs are finite; a program needn't handle non-finite values.
Results may differ from a plain program's by a relative error of at most 0.0003.
Values may be sent and summed in bfloat16 or wider, within the bound.
No kernel may reach another device: no remote copies, remote signals or barrier semaphores. Data moves between devices by JAX's collectives and lax.ppermute only.
A program may use at most 128 MiB of HBM per device.

v0:
```python
import math
import jax
import jax.numpy as jnp
from jax import lax
from jax.sharding import PartitionSpec as P

P_SIZE = 16384
PANEL = 128
PANELS = 2


def broadcast(x, axis, root):
    mine = lax.axis_index(axis) == root
    return lax.psum(jnp.where(mine, x, jnp.zeros_like(x)), axis)


def on_device(features, queries, damping):
    rows_here = damping.shape[0]
    cols_here = queries.shape[1]
    slab_total = features.shape[0] * lax.axis_size("wide")
    wide_pos = lax.axis_index("wide")
    narrow_pos = lax.axis_index("narrow")
    contract_rows = (((0,), (0,)), ((), ()))
    contract_cols = (((1,), (1,)), ((), ()))
    full_width = lax.all_gather(features, "narrow", axis=1, tiled=True)
    row_features = lax.all_to_all(full_width, "wide", split_axis=1, concat_axis=0, tiled=True)
    slab_columns = lax.all_gather(features, "wide", axis=0, tiled=True)
    products = lax.dot_general(
        row_features, slab_columns, contract_rows, preferred_element_type=jnp.float32
    )
    partial_value = lax.dot_general(
        queries, slab_columns, contract_cols, preferred_element_type=jnp.float32
    )
    scores = lax.psum_scatter(partial_value, "narrow", scatter_dimension=1, tiled=True) * (
        1.0 / math.sqrt(P_SIZE)
    )
    row_ids = wide_pos * rows_here + lax.broadcasted_iota(jnp.int32, (rows_here, 1), 0)
    col_ids = narrow_pos * cols_here + lax.broadcasted_iota(jnp.int32, (1, cols_here), 1)
    kernel_block = products / slab_total + jnp.where(
        row_ids == col_ids, damping[:, None], jnp.float32(0.0)
    )
    factors = []
    for panel_index in range(PANELS):
        offset = panel_index * PANEL
        column_root = offset // cols_here
        row_root = offset // rows_here
        col_shift = offset % cols_here
        row_shift = offset % rows_here
        panel_columns = broadcast(
            kernel_block[:, col_shift : col_shift + PANEL], "narrow", column_root
        )
        pivot_block = broadcast(panel_columns[row_shift : row_shift + PANEL], "wide", row_root)
        pivot_factor = jnp.linalg.cholesky(pivot_block)
        lower_rows = lax.linalg.triangular_solve(
            pivot_factor, panel_columns, left_side=False, lower=True, transpose_a=True
        )
        pivot_rows = broadcast(kernel_block[row_shift : row_shift + PANEL], "wide", row_root)
        lower_cols = lax.linalg.triangular_solve(
            pivot_factor, pivot_rows, left_side=True, lower=True, transpose_a=False
        ).T
        kernel_block = kernel_block - jnp.dot(
            lower_rows,
            lower_cols.T,
            precision=lax.Precision.HIGHEST,
            preferred_element_type=jnp.float32,
        )
        boundary = offset + PANEL
        kernel_block = jnp.where(
            (row_ids < boundary) | (col_ids < boundary), jnp.zeros_like(kernel_block), kernel_block
        )
        factors.append(lower_rows)
    return (kernel_block, jnp.concatenate(factors, axis=1), scores)


def solution(mesh):
    return jax.shard_map(
        on_device,
        mesh=mesh,
        in_specs=(P("wide", "narrow"), P("wide", "narrow"), P("wide")),
        out_specs=(P("wide", "narrow"), P("wide", None), P("wide", "narrow")),
        check_vma=False,
    )
```

profile of v0, /device:TPU:0, one launch (start us, length us, event | category | flops | bytes accessed | tf_op | source)
XLA Modules:
  0.0 752.9 jit_solution(7625984602944274443)
XLA Ops:
  8.7 12.7 %all-gather.3.cloned.1.call-done = bf16[32,16384]{1,0:T(8,128)(2,1)} async-done(((bf16[32,8192]{1,0:T(8,128)(2,1)}), bf16[32,16384]{1,0:T(8,128)(2,1)}) %all-gather.3.cloned.1.call-update) | async-done | bytes 1048592 | tf_op jit(solution)/shard_map/all_gather | solution.py:25
  21.3 2.3 copy.41
  23.6 6.8 all-to-all-start
  30.5 35.8 %all-to-all-done = bf16[32,16,1024]{2,0,1:T(8,128)(2,1)S(1)} async-done(((bf16[32,16,1024]{2,0,1:T(8,128)(2,1)}), bf16[32,16,1024]{2,0,1:T(8,128)(2,1)S(1)}, u32[]{:S(2)}, u32[]{:S(2)}) %all-to-all-start) | async-done | bytes 1048608 | tf_op jit(solution)/shard_map/all_to_all | solution.py:26
  66.3 85.7 %all-gather.5.cloned.1.call-done = bf16[512,8192]{1,0:T(8,128)(2,1)} async-done(((bf16[32,8192]{1,0:T(8,128)(2,1)}), bf16[512,8192]{1,0:T(8,128)(2,1)}) %all-gather.5.cloned.1.call-update) | async-done | bytes 8388624 | tf_op jit(solution)/shard_map/all_gather | solution.py:27
  151.9 19.3 %select_add_fusion = f32[1024,8192]{0,1:T(8,128)} fusion(bf16[512,1024]{1,0:T(8,128)(2,1)S(1)} %bitcast.49, bf16[512,8192]{1,0:T(8,128)(2,1)} %all-gather.5.cloned.1.call-done, f32[1024]{0:T(1024)} %param.10, s32[1024]{0:T(1024)S(1)} %iota_add_fusion.1, s32[8192]{0:T(1024)S(1)} %iota_add_fusion), kind=kOutput, calls=%fused_computation.2 | convolution fusion | flops 8623489024 | bytes 43032576 | tf_op jit(solution)/shard_map/dot_general | solution.py:28
  171.3 1.9 slice_select_fusion.3
  173.2 4.4 slice_select_fusion.1
  177.6 12.5 %all-reduce.7.cloned.1.call-done = f32[1024,128]{0,1:T(8,128)} async-done(((f32[1024,128]{0,1:T(8,128)}), f32[1024,128]{0,1:T(8,128)}) %all-reduce.7.cloned.1.call-update) | async-done | bytes 524304 | tf_op jit(solution)/shard_map/psum | solution.py:14
  190.1 1.5 slice_select_fusion.5
  192.1 175.9 %all-reduce.13.cloned.1.call-done = (f32[128,128]{0,1:T(8,128)}, f32[128,8192]{0,1:T(8,128)}) async-done(((f32[128,128]{0,1:T(8,128)}, f32[128,8192]{0,1:T(8,128)}), (f32[128,128]{0,1:T(8,128)}, f32[128,8192]{0,1:T(8,128)})) %all-reduce.13.cloned.1.call-update) | async-done | bytes 4259856 | tf_op jit(solution)/shard_map/psum | solution.py:14
  368.0 0.9 copy.30
  368.9 0.9 fusion.9
  369.7 11.7 %cholesky.44 = f32[128,128]{1,0:T(8,128)S(1)} custom-call(f32[128,128]{1,0:T(8,128)S(1)} %fusion.9), custom_call_target="Cholesky" | custom-call | tf_op jit(solution)/shard_map/jit(cholesky)/cholesky | solution.py:53
  382.8 9.8 %custom-call.10 = f32[1,128,128]{1,2,0:T(8,128)S(1)} custom-call(f32[1,128,128]{2,1,0:T(8,128)S(1)} %fusion), custom_call_target="InvertDiagBlocksLowerTriangular" | custom-call | tf_op jit(solution)/shard_map/triangular_solve/custom-call.0 | solution.py:54
  392.6 6.1 fusion.6
  399.3 35.1 %subtract_select_fusion.1 = f32[1024,8192]{0,1:T(8,128)} fusion(f32[1024,8192]{0,1:T(8,128)} %select_add_fusion, f32[1024,128]{0,1:T(8,128)S(1)} %convolution_bitcast_fusion.1, f32[128,8192]{1,0:T(8,128)S(1)} %fusion.6, pred[1024]{0:T(1024)(128)(4,1)S(1)} %fusion.12, pred[8192]{0:T(1024)(128)(4,1)S(1)} %fusion.10), kind=kOutput, calls=%fused_computation.1 | convolution fusion | flops 12910067712 | bytes 71836672 | tf_op jit(solution)/shard_map/dot_general | solution.py:61
  434.5 1.9 slice_select_fusion.2
  436.4 6.7 fusion.14
  443.4 4.4 slice_select_fusion
  447.8 6.4 all-reduce.9.cloned.1.call-done
  454.2 1.5 slice_select_fusion.4
  455.8 9.3 %reduce-scatter.2.cloned.1.call-done = f32[64,256]{1,0:T(8,128)} async-done(((f32[64,512]{1,0:T(8,128)}), f32[64,256]{1,0:T(8,128)}) %reduce-scatter.2.cloned.1.call-update) | async-done | bytes 65552 | tf_op jit(solution)/shard_map/reduce_scatter | solution.py:34
  465.1 1.5 broadcast_multiply_fusion
  466.5 176.4 %all-reduce.11.cloned.1.call-done = (f32[128,128]{0,1:T(8,128)}, f32[128,8192]{0,1:T(8,128)}) async-done(((f32[128,128]{0,1:T(8,128)}, f32[128,8192]{0,1:T(8,128)}), (f32[128,128]{0,1:T(8,128)}, f32[128,8192]{0,1:T(8,128)})) %all-reduce.11.cloned.1.call-update) | async-done | bytes 4259856 | tf_op jit(solution)/shard_map/psum | solution.py:14
  643.0 0.9 copy.32
  644.7 11.7 %cholesky.55 = f32[128,128]{1,0:T(8,128)S(1)} custom-call(f32[128,128]{1,0:T(8,128)S(1)} %fusion.5), custom_call_target="Cholesky" | custom-call | tf_op jit(solution)/shard_map/jit(cholesky)/cholesky | solution.py:53
  657.8 9.8 %custom-call.12 = f32[1,128,128]{1,2,0:T(8,128)S(1)} custom-call(f32[1,128,128]{2,1,0:T(8,128)S(1)} %fusion.1), custom_call_target="InvertDiagBlocksLowerTriangular" | custom-call | tf_op jit(solution)/shard_map/triangular_solve/custom-call.0 | solution.py:54
  667.6 8.0 %fusion.2 = f32[128,8192]{1,0:T(8,128)} fusion(f32[128,8192]{0,1:T(8,128)} %get-tuple-element.19, f32[1,128,128]{1,2,0:T(8,128)S(1)} %custom-call.12), kind=kOutput, calls=%fused_computation.17 | convolution fusion | flops 1610612736 | bytes 8454144 | tf_op jit(solution)/shard_map/triangular_solve/dot.0 | solution.py:58
  676.3 1.3 copy.35
  677.7 37.0 %subtract_select_fusion = f32[1024,8192]{0,1:T(8,128)} fusion(f32[1024,8192]{0,1:T(8,128)} %subtract_select_fusion.1, f32[1024,128]{0,1:T(8,128)S(1)} %convolution_bitcast_fusion, f32[128,8192]{1,0:T(8,128)} %fusion.2, pred[1024]{0:T(1024)(128)(4,1)S(1)} %fusion.13, pred[8192]{0:T(1024)(128)(4,1)S(1)} %fusion.11), kind=kOutput, calls=%fused_computation | convolution fusion | flops 12910067712 | bytes 71836672 | tf_op jit(solution)/shard_map/dot_general | solution.py:61
  714.6 31.2 %copy.34 = f32[1024,8192]{1,0:T(8,128)} copy(f32[1024,8192]{0,1:T(8,128)} %subtract_select_fusion) | data formatting | bytes 67108864
  (38 shorter events, 7.1 us)
Async XLA Ops:
  7.2 429.3 %copy-start = (bf16[64,8192]{1,0:T(8,128)(2,1)S(1)}, bf16[64,8192]{1,0:T(8,128)(2,1)}, u32[]{:S(2)}) copy-start(bf16[64,8192]{1,0:T(8,128)(2,1)} %param.9) | copy-start | bytes 3145732
  7.2 14.1 %all-gather.3.cloned.1.call-start = ((), (), s32[]{:S(2)}) async-start(), calls=%async_computation.2 | async-start | bytes 1572864 | tf_op jit(solution)/shard_map/all_gather | solution.py:25
  7.9 144.0 %all-gather.5.cloned.1.call-start = ((), (), s32[]{:S(2)}) async-start(), calls=%async_computation.3 | async-start | bytes 8912896 | tf_op jit(solution)/shard_map/all_gather | solution.py:27
  23.6 42.7 %all-to-all-start = ((bf16[32,16,1024]{2,0,1:T(8,128)(2,1)}), bf16[32,16,1024]{2,0,1:T(8,128)(2,1)S(1)}, u32[]{:S(2)}, u32[]{:S(2)}) async-start(bf16[32,16,1024]{2,0,1:T(8,128)(2,1)} %bitcast.48), calls=%async_computation | async-start | bytes 2097152 | tf_op jit(solution)/shard_map/all_to_all | solution.py:26
  30.4 159.7 %all-reduce.7.cloned.1.call-start = ((), (), s32[]{:S(2)}) async-start(), calls=%async_computation.4 | async-start | bytes 1048576 | tf_op jit(solution)/shard_map/psum | solution.py:14
  173.2 194.8 %all-reduce.13.cloned.1.call-start = ((), (), s32[]{:S(2)}) async-start(), calls=%async_computation.8 | async-start | bytes 8519680 | tf_op jit(solution)/shard_map/psum | solution.py:14
  190.1 208.6 %copy-start.3 = (f32[1024,128]{0,1:T(8,128)S(1)}, f32[1024,128]{0,1:T(8,128)}, u32[]{:S(2)}) copy-start(f32[1024,128]{0,1:T(8,128)} %all-reduce.7.cloned.1.call-done) | copy-start | bytes 1572868
  191.7 262.5 %all-reduce.9.cloned.1.call-start = ((), (), s32[]{:S(2)}) async-start(), calls=%async_computation.5 | async-start | bytes 1048576 | tf_op jit(solution)/shard_map/psum | solution.py:14
  436.4 28.7 %reduce-scatter.2.cloned.1.call-start = ((), (), s32[]{:S(2)}) async-start(), calls=%async_computation.6 | async-start | bytes 196608 | tf_op jit(solution)/shard_map/reduce_scatter | solution.py:34
  443.2 199.8 %all-reduce.11.cloned.1.call-start = ((), (), s32[]{:S(2)}) async-start(), calls=%async_computation.7 | async-start | bytes 8519680 | tf_op jit(solution)/shard_map/psum | solution.py:14
  454.2 221.4 %copy-start.2 = (f32[1024,128]{0,1:T(8,128)S(1)}, f32[1024,128]{0,1:T(8,128)}, u32[]{:S(2)}) copy-start(f32[1024,128]{0,1:T(8,128)} %all-reduce.9.cloned.1.call-done) | copy-start | bytes 1572868
  714.6 31.2 %copy-start.1 = (bf16[64,8192]{1,0:T(8,128)(2,1)S(1)}, bf16[64,8192]{1,0:T(8,128)(2,1)}, u32[]{:S(2)}) copy-start(bf16[64,8192]{1,0:T(8,128)(2,1)} %param.9) | copy-start | bytes 3145732
Sparse Core Ops, SparseCore 0:
  9.5 11.7 all-gather.2
  24.1 127.8 all-gather.4
  173.3 16.7 all-reduce.6
  196.5 171.4 all-reduce.12
  436.5 17.6 all-reduce.8
  456.2 8.7 reduce-scatter.1
  471.6 171.3 all-reduce.10
where the time goes:
time: 759 us; the launch traced here: 753 us
  waiting for transfers between devices  516 us (68%)
  matrix products  113 us (15%)
  other arithmetic  64.7 us (9%)
  local copies, waits for them, and re-layouts  36.6 us (5%)
  between operations  14.5 us (2%)
    psum x4, waiting for transfers between devices, broadcast(): return lax.psum(jnp.where(mine, x, jnp.zeros_like(x)), axis)  371 us
    all_gather x1, waiting for transfers between devices, on_device(): slab_columns = lax.all_gather(features, 'wide', axis=0, tiled=True)  85.7 us
    dot_general x2, matrix products, on_device(): jnp.dot(lower_rows, lower_cols.T, precision=lax.Precision.HIGHEST, prefer...  72.1 us
    all_to_all x1, waiting for transfers between devices, on_device(): lax.all_to_all(full_width, 'wide', split_axis=1, concat_axis=0, tiled=True)  35.8 us
    unnamed x10, local copies, waits for them, and re-layouts  32.5 us
    another operation x6, other arithmetic, on_device(): pivot_factor = jnp.linalg.cholesky(pivot_block)  24.8 us
    another operation x4, other arithmetic, on_device(): lax.linalg.triangular_solve(pivot_factor, panel_columns, left_side=False,...  20.9 us
    dot_general x1, matrix products, on_device(): lax.dot_general(row_features, slab_columns, contract_rows, preferred_elem...  19.3 us
  transfers between devices with their start and end apart: 8, of which 8 were waited for; matrix products, arithmetic and copies ran while one was open for 3% of the time, Pallas kernels for 0%

commit v1 on v0

--- a/solution.py
+++ b/solution.py
@@ -1,3 +1,4 @@
+import functools
 import math
 import jax
 import jax.numpy as jnp
@@ -7,6 +8,17 @@
 P_SIZE = 16384
 PANEL = 128
 PANELS = 2
+
+
+def _rest_view(x_part, d0):
+    far_arr = jnp.stack([x_part for _ in range(lax.psum(1, axis_name="wide"))], axis=0)
+    reply = jnp.concatenate(
+        lax.all_to_all(far_arr, axis_name="wide", split_axis=0, concat_axis=0), d0
+    )
+    return reply
+
+
+link_the_local_data = functools.partial(_rest_view, d0=0)
 
 
 def broadcast(x, axis, root):
@@ -24,7 +36,7 @@
     contract_cols = (((1,), (1,)), ((), ()))
     full_width = lax.all_gather(features, "narrow", axis=1, tiled=True)
     row_features = lax.all_to_all(full_width, "wide", split_axis=1, concat_axis=0, tiled=True)
-    slab_columns = lax.all_gather(features, "wide", axis=0, tiled=True)
+    slab_columns = link_the_local_data(features)
     products = lax.dot_general(
         row_features, slab_columns, contract_rows, preferred_element_type=jnp.float32
     )

time: 759 us -> 863 us (1.14)
  waiting for transfers between devices: 516 us -> 583 us
  blocking collectives: 0 us -> 33.3 us
    all_to_all x1, waiting for transfers between devices: 35.8 us -> 153 us  [_rest_view(): lax.all_to_all(far_arr, axis_name='wide', split_axis=0, concat_axis=0)]
    all_gather x1 -> x0, waiting for transfers between devices: 85.7 us -> none  [on_device(): slab_columns = lax.all_gather(features, 'wide', axis=0, tiled=True)]
    psum x4, waiting for transfers between devices: 371 us -> 407 us  [broadcast(): return lax.psum(jnp.where(mine, x, jnp.zeros_like(x)), axis)]
    all_to_all x0 -> x1, blocking collectives: none -> 33.3 us  [on_device(): lax.all_to_all(full_width, 'wide', split_axis=1, concat_axis=0, tiled=True)]
    unnamed x10 -> x12, local copies, waits for them, and re-layouts: 32.5 us -> 32.5 us
  transfers between devices with their start and end apart: 8 -> 7, of which waited for: 8 -> 7; matrix products, arithmetic and copies ran while one was open for 3% -> 2% of each run, Pallas kernels for 0% -> 0%
where the time goes in v1:
time: 863 us; the launch traced here: 856 us
  waiting for transfers between devices  583 us (68%)
  matrix products  114 us (13%)
  other arithmetic  64.7 us (7%)
  local copies, waits for them, and re-layouts  41.1 us (5%)
  blocking collectives  33.3 us (4%)
  between operations  14.5 us (2%)
    psum x4, waiting for transfers between devices, broadcast(): return lax.psum(jnp.where(mine, x, jnp.zeros_like(x)), axis)  407 us
    all_to_all x1, waiting for transfers between devices, _rest_view(): lax.all_to_all(far_arr, axis_name='wide', split_axis=0, concat_axis=0)  153 us
    dot_general x2, matrix products, on_device(): jnp.dot(lower_rows, lower_cols.T, precision=lax.Precision.HIGHEST, prefer...  72.1 us
    all_to_all x1, blocking collectives, on_device(): lax.all_to_all(full_width, 'wide', split_axis=1, concat_axis=0, tiled=True)  33.3 us
    unnamed x12, local copies, waits for them, and re-layouts  32.5 us
    another operation x6, other arithmetic, on_device(): pivot_factor = jnp.linalg.cholesky(pivot_block)  24.8 us
    another operation x4, other arithmetic, on_device(): lax.linalg.triangular_solve(pivot_factor, panel_columns, left_side=False,...  20.9 us
    dot_general x1, matrix products, on_device(): lax.dot_general(row_features, slab_columns, contract_rows, preferred_elem...  19.4 us
  transfers between devices with their start and end apart: 7, of which 7 were waited for; matrix products, arithmetic and copies ran while one was open for 2% of the time, Pallas kernels for 0%

profile of v1, /device:TPU:0, one launch (start us, length us, event | category | flops | bytes accessed | tf_op | source)
XLA Modules:
  0.0 856.1 jit_solution(12248012027570586367)
XLA Ops:
  7.9 13.4 %all-gather.2.cloned.1.call-done = bf16[32,16384]{1,0:T(8,128)(2,1)} async-done(((bf16[32,8192]{1,0:T(8,128)(2,1)}), bf16[32,16384]{1,0:T(8,128)(2,1)}) %all-gather.2.cloned.1.call-update) | async-done | bytes 1048592 | tf_op jit(solution)/shard_map/all_gather | solution.py:37
  21.3 1.3 copy.27
  22.6 33.3 %all_to_all.21 = bf16[32,16,1024]{2,0,1:T(8,128)(2,1)S(1)} all-to-all(bf16[32,16,1024]{2,0,1:T(8,128)(2,1)S(1)} %bitcast.53), channel_id=1, replica_groups=mesh['wide'=16,'narrow'=2] {'wide'}, dimensions={1} | all-to-all | bytes 2097152 | tf_op jit(solution)/shard_map/all_to_all | solution.py:38
  55.9 5.5 stack.2
  61.4 4.9 all-to-all-start.1
  66.4 153.3 %all-to-all-done.1 = bf16[16,32,8192]{2,1,0:T(8,128)(2,1)} async-done(((bf16[16,32,8192]{2,1,0:T(8,128)(2,1)}), bf16[16,32,8192]{2,1,0:T(8,128)(2,1)}, u32[]{:S(2)}, u32[]{:S(2)}) %all-to-all-start.1) | async-done | bytes 8388640 | tf_op jit(solution)/shard_map/all_to_all | solution.py:16
  219.7 19.4 %fusion = f32[1024,8192]{0,1:T(8,128)} fusion(bf16[16,32,8192]{2,1,0:T(8,128)(2,1)} %all-to-all-done.1, f32[1024]{0:T(1024)S(1)} %copy-done.4, s32[1024]{0:T(1024)S(1)} %iota_add_fusion.1, s32[8192]{0:T(1024)S(1)} %iota_add_fusion, bf16[32,16,1024]{2,0,1:T(8,128)(2,1)S(1)} %all_to_all.21), kind=kOutput, calls=%fused_computation.1 | convolution fusion | flops 8623489024 | bytes 43032576 | tf_op jit(solution)/shard_map/dot_general | solution.py:40
  239.1 1.9 slice_select_fusion.3
  241.0 4.4 slice_select_fusion.1
  245.4 47.9 %all-reduce.7.cloned.1.call-done = f32[1024,128]{0,1:T(8,128)} async-done(((f32[1024,128]{0,1:T(8,128)}), f32[1024,128]{0,1:T(8,128)}) %all-reduce.7.cloned.1.call-update) | async-done | bytes 524304 | tf_op jit(solution)/shard_map/psum | solution.py:26
  293.4 1.5 slice_select_fusion.5
  295.3 176.0 %all-reduce.13.cloned.1.call-done = (f32[128,128]{0,1:T(8,128)}, f32[128,8192]{0,1:T(8,128)}) async-done(((f32[128,128]{0,1:T(8,128)}, f32[128,8192]{0,1:T(8,128)}), (f32[128,128]{0,1:T(8,128)}, f32[128,8192]{0,1:T(8,128)})) %all-reduce.13.cloned.1.call-update) | async-done | bytes 4259856 | tf_op jit(solution)/shard_map/psum | solution.py:26
  471.3 0.9 copy.15
  473.1 11.7 %cholesky.44 = f32[128,128]{1,0:T(8,128)S(1)} custom-call(f32[128,128]{1,0:T(8,128)S(1)} %fusion.11), custom_call_target="Cholesky" | custom-call | tf_op jit(solution)/shard_map/jit(cholesky)/cholesky | solution.py:65
  486.2 9.8 %custom-call.10 = f32[1,128,128]{1,2,0:T(8,128)S(1)} custom-call(f32[1,128,128]{2,1,0:T(8,128)S(1)} %fusion.2), custom_call_target="InvertDiagBlocksLowerTriangular" | custom-call | tf_op jit(solution)/shard_map/triangular_solve/custom-call.0 | solution.py:66
  496.0 6.1 fusion.8
  502.7 35.1 %subtract_select_fusion.1 = f32[1024,8192]{0,1:T(8,128)} fusion(f32[1024,8192]{0,1:T(8,128)} %fusion, f32[1024,128]{0,1:T(8,128)S(1)} %convolution_bitcast_fusion.1, f32[128,8192]{1,0:T(8,128)S(1)} %fusion.8, pred[1024]{0:T(1024)(128)(4,1)S(1)} %fusion.14, pred[8192]{0:T(1024)(128)(4,1)S(1)} %fusion.12), kind=kOutput, calls=%fused_computation.3 | convolution fusion | flops 12910067712 | bytes 71836672 | tf_op jit(solution)/shard_map/dot_general | solution.py:73
  537.9 1.9 slice_select_fusion.2
  539.8 6.7 fusion.16
  546.8 4.4 slice_select_fusion
  551.2 6.3 all-reduce.9.cloned.1.call-done
  557.6 1.5 slice_select_fusion.4
  559.2 9.3 %reduce-scatter.2.cloned.1.call-done = f32[64,256]{1,0:T(8,128)} async-done(((f32[64,512]{1,0:T(8,128)}), f32[64,256]{1,0:T(8,128)}) %reduce-scatter.2.cloned.1.call-update) | async-done | bytes 65552 | tf_op jit(solution)/shard_map/reduce_scatter | solution.py:46
  568.4 1.5 broadcast_multiply_fusion
  569.9 176.3 %all-reduce.11.cloned.1.call-done = (f32[128,128]{0,1:T(8,128)}, f32[128,8192]{0,1:T(8,128)}) async-done(((f32[128,128]{0,1:T(8,128)}, f32[128,8192]{0,1:T(8,128)}), (f32[128,128]{0,1:T(8,128)}, f32[128,8192]{0,1:T(8,128)})) %all-reduce.11.cloned.1.call-update) | async-done | bytes 4259856 | tf_op jit(solution)/shard_map/psum | solution.py:26
  746.2 0.9 copy.17
  748.0 11.7 %cholesky.55 = f32[128,128]{1,0:T(8,128)S(1)} custom-call(f32[128,128]{1,0:T(8,128)S(1)} %fusion.7), custom_call_target="Cholesky" | custom-call | tf_op jit(solution)/shard_map/jit(cholesky)/cholesky | solution.py:65
  761.0 9.8 %custom-call.12 = f32[1,128,128]{1,2,0:T(8,128)S(1)} custom-call(f32[1,128,128]{2,1,0:T(8,128)S(1)} %fusion.3), custom_call_target="InvertDiagBlocksLowerTriangular" | custom-call | tf_op jit(solution)/shard_map/triangular_solve/custom-call.0 | solution.py:66
  770.8 8.0 fusion.4
  779.6 1.3 copy.20
  780.9 37.0 %subtract_select_fusion = f32[1024,8192]{0,1:T(8,128)} fusion(f32[1024,8192]{0,1:T(8,128)} %subtract_select_fusion.1, f32[1024,128]{0,1:T(8,128)S(1)} %convolution_bitcast_fusion, f32[128,8192]{1,0:T(8,128)} %fusion.4, pred[1024]{0:T(1024)(128)(4,1)S(1)} %fusion.15, pred[8192]{0:T(1024)(128)(4,1)S(1)} %fusion.13), kind=kOutput, calls=%fused_computation.2 | convolution fusion | flops 12910067712 | bytes 71836672 | tf_op jit(solution)/shard_map/dot_general | solution.py:73
  817.8 31.2 %copy.19 = f32[1024,8192]{1,0:T(8,128)} copy(f32[1024,8192]{0,1:T(8,128)} %subtract_select_fusion) | data formatting | bytes 67108864
  (39 shorter events, 7.3 us)
Async XLA Ops:
  7.2 532.7 %copy-start = (bf16[64,8192]{1,0:T(8,128)(2,1)S(1)}, bf16[64,8192]{1,0:T(8,128)(2,1)}, u32[]{:S(2)}) copy-start(bf16[64,8192]{1,0:T(8,128)(2,1)} %param.9) | copy-start | bytes 3145732
  7.2 14.1 %all-gather.2.cloned.1.call-start = ((), (), s32[]{:S(2)}) async-start(), calls=%async_computation.3 | async-start | bytes 1572864 | tf_op jit(solution)/shard_map/all_gather | solution.py:37
  61.4 158.2 %copy-start.4 = (f32[1024]{0:T(1024)S(1)}, f32[1024]{0:T(1024)}, u32[]{:S(2)}) copy-start(f32[1024]{0:T(1024)} %param.10) | copy-start | bytes 12292
  61.4 158.2 %all-to-all-start.1 = ((bf16[16,32,8192]{2,1,0:T(8,128)(2,1)}), bf16[16,32,8192]{2,1,0:T(8,128)(2,1)}, u32[]{:S(2)}, u32[]{:S(2)}) async-start(bf16[16,32,8192]{2,1,0:T(8,128)(2,1)} %stack.2), calls=%async_computation.1 | async-start | bytes 16777216 | tf_op jit(solution)/shard_map/all_to_all | solution.py:16
  66.3 227.0 %all-reduce.7.cloned.1.call-start = ((), (), s32[]{:S(2)}) async-start(), calls=%async_computation.4 | async-start | bytes 1048576 | tf_op jit(solution)/shard_map/psum | solution.py:26
  241.0 230.4 %all-reduce.13.cloned.1.call-start = ((), (), s32[]{:S(2)}) async-start(), calls=%async_computation.8 | async-start | bytes 8519680 | tf_op jit(solution)/shard_map/psum | solution.py:26
  293.4 208.7 %copy-start.3 = (f32[1024,128]{0,1:T(8,128)S(1)}, f32[1024,128]{0,1:T(8,128)}, u32[]{:S(2)}) copy-start(f32[1024,128]{0,1:T(8,128)} %all-reduce.7.cloned.1.call-done) | copy-start | bytes 1572868
  294.9 262.6 %all-reduce.9.cloned.1.call-start = ((), (), s32[]{:S(2)}) async-start(), calls=%async_computation.5 | async-start | bytes 1048576 | tf_op jit(solution)/shard_map/psum | solution.py:26
  539.8 28.7 %reduce-scatter.2.cloned.1.call-start = ((), (), s32[]{:S(2)}) async-start(), calls=%async_computation.6 | async-start | bytes 196608 | tf_op jit(solution)/shard_map/reduce_scatter | solution.py:46
  546.5 199.6 %all-reduce.11.cloned.1.call-start = ((), (), s32[]{:S(2)}) async-start(), calls=%async_computation.7 | async-start | bytes 8519680 | tf_op jit(solution)/shard_map/psum | solution.py:26
  557.5 221.3 %copy-start.2 = (f32[1024,128]{0,1:T(8,128)S(1)}, f32[1024,128]{0,1:T(8,128)}, u32[]{:S(2)}) copy-start(f32[1024,128]{0,1:T(8,128)} %all-reduce.9.cloned.1.call-done) | copy-start | bytes 1572868
  817.8 31.2 %copy-start.1 = (bf16[64,8192]{1,0:T(8,128)(2,1)S(1)}, bf16[64,8192]{1,0:T(8,128)(2,1)}, u32[]{:S(2)}) copy-start(bf16[64,8192]{1,0:T(8,128)(2,1)} %param.9) | copy-start | bytes 3145732
Sparse Core Ops, SparseCore 0:
  9.5 11.7 all-gather.1
  241.1 52.2 all-reduce.6
  299.9 171.4 all-reduce.12
  539.9 17.6 all-reduce.8
  559.6 8.7 reduce-scatter.1
  574.8 171.3 all-reduce.10
